TPU v7x, 32 devices: a whole 2x2x4 slice. The times are simulated.
32 devices in a mesh: tp: 4 (over y, x), dp: 8 (over z, core).
Axes of the slice: x: 2, y: 2, z: 4, core: 2. Of those that a mesh axis runs over, the one named last changes fastest.
Arguments:
- activations: bfloat16 [2, 8192, 8192], P(None, 'dp', 'tp'), may hold values from -72 to 72
- out_grads: bfloat16 [2, 8192, 2048], P(None, 'dp'), may hold values from -2 to 2
- master: float32 [8192, 2, 2048], P(('tp', 'dp')), may hold values from -1.2 to 1.2
- first_moment: float32 [8192, 2, 2048], P(('tp', 'dp')), may hold values from -1.8 to 1.8
- second_moment: float32 [8192, 2, 2048], P(('tp', 'dp')), may hold values from 0.01 to 1
Outputs:
- new_master: float32 [8192, 2, 2048], P(('tp', 'dp'))
- new_first: float32 [8192, 2, 2048], P(('tp', 'dp'))
- new_second: float32 [8192, 2, 2048], P(('tp', 'dp'))
- weights: bfloat16 [8192, 2, 2048], P('tp')
All inputs are finite; a program needn't handle non-finite values.
Results may differ from a plain program's by a relative error of at most 0.0004.
Values may be sent and summed in bfloat16 or wider, within the bound.
A program may use at most 192 MiB of HBM per device.

v0:
```python
import math

import jax
import jax.numpy as jnp
from jax import lax
from jax.sharding import PartitionSpec as P

beta_first = 0.9
beta_second = 0.95
first_fix = 1.0 - 0.9**10
second_fix = 1.0 - 0.95**10
learn_rate = 0.01
decay_rate = 0.1
epsilon = 1e-08
limit_scale = 2.0


def reduce_rows(layer_acts, layer_grads):
    grad_own = lax.psum_scatter(
        jnp.einsum("ltr,ltc->rlc", layer_acts, layer_grads, preferred_element_type=jnp.float32),
        "dp",
        scatter_dimension=0,
        tiled=True,
    )
    partial_value = jnp.sum(grad_own * grad_own)
    return (grad_own, partial_value)


def adam_update(grad_own, master, first_moment, second_moment, clip_factor):
    clipped = clip_factor * grad_own
    new_first = beta_first * first_moment + (1.0 - beta_first) * clipped
    new_second = beta_second * second_moment + (1.0 - beta_second) * clipped * clipped
    step_dir = new_first / first_fix / (jnp.sqrt(new_second / second_fix) + epsilon)
    new_master = master - learn_rate * (step_dir + decay_rate * master)
    return (new_master, new_first, new_second)


def on_device(activations, out_grads, master, first_moment, second_moment):
    own_rows = master.shape[0]
    grad_own, layer_sum = reduce_rows(activations, out_grads)
    sum_squares = lax.psum(layer_sum, ("tp", "dp"))
    entries = (
        own_rows * lax.axis_size("tp") * lax.axis_size("dp") * master.shape[1] * master.shape[2]
    )
    limit = limit_scale * math.sqrt(entries)
    clip_factor = limit / jnp.maximum(jnp.sqrt(sum_squares), limit)
    new_master, new_first, new_second = adam_update(
        grad_own, master, first_moment, second_moment, clip_factor
    )
    rounded = new_master.astype(jnp.bfloat16)
    tp_rows = lax.all_gather(rounded, "dp", axis=0, tiled=True)
    return (new_master, new_first, new_second, tp_rows)


def solution(mesh):
    return jax.shard_map(
        on_device,
        mesh=mesh,
        in_specs=(
            P(None, "dp", "tp"),
            P(None, "dp", None),
            P(("tp", "dp"), None, None),
            P(("tp", "dp"), None, None),
            P(("tp", "dp"), None, None),
        ),
        out_specs=(
            P(("tp", "dp"), None, None),
            P(("tp", "dp"), None, None),
            P(("tp", "dp"), None, None),
            P("tp", None, None),
        ),
        check_vma=False,
    )
```

profile of v0, /device:TPU:0, one launch (start us, length us, event | category | flops | bytes accessed | tf_op | source)
XLA Modules:
  0.0 623.6 jit_solution(12652880110053405186)
XLA Ops:
  7.2 0.0 reduce-scatter.2.cloned.1.call-start
  7.2 25.6 %convolution_bitcast_fusion = f32[2048,2,2048]{0,2,1:T(8,128)} fusion(bf16[2,1024,2048]{2,1,0:T(8,128)(2,1)} %param.6, bf16[2,1024,2048]{2,1,0:T(8,128)(2,1)} %param.5), kind=kOutput, calls=%fused_computation | convolution fusion | flops 17179869184 | bytes 50331648 | tf_op jit(solution)/shard_map/ltr,ltc->rlc/dot_general | solution.py:20
  32.9 0.0 reduce-scatter.2.cloned.1.call-update
  32.9 0.0 all-gather.2.cloned.1.call-start
  32.9 7.2 %copy.13 = f32[256,2,2048]{0,2,1:T(8,128)} copy(f32[256,2,2048]{2,1,0:T(2,128)} %param.7) | data formatting | bytes 8388608 | tf_op args[2]
  40.1 7.2 %copy.9 = f32[256,2,2048]{0,2,1:T(8,128)} copy(f32[256,2,2048]{2,1,0:T(2,128)} %param.8) | data formatting | bytes 8388608 | tf_op args[3]
  47.4 313.8 %reduce-scatter.2.cloned.1.call-done = f32[256,2,2048]{0,2,1:T(8,128)} async-done(((f32[2048,2,2048]{0,2,1:T(8,128)}), f32[256,2,2048]{0,2,1:T(8,128)}) %reduce-scatter.2.cloned.1.call-update) | async-done | bytes 4194320 | tf_op jit(solution)/shard_map/reduce_scatter | solution.py:19
  361.2 3.9 multiply_reduce_fusion
  365.1 7.2 %copy.11 = f32[256,2,2048]{0,2,1:T(8,128)} copy(f32[256,2,2048]{2,1,0:T(2,128)} %param.9) | data formatting | bytes 8388608 | tf_op args[4]
  372.3 37.9 %psum.7 = f32[]{:T(128)} all-reduce(f32[]{:T(128)} %multiply_reduce_fusion), channel_id=1, replica_groups=mesh['tp'=4,'dp'=8] {'tp','dp'}, use_global_device_ids=true, to_apply=%region_2.0 | all-reduce | flops 1 | bytes 8 | tf_op jit(solution)/shard_map/psum | solution.py:41
  411.0 11.7 %fusion.1 = (bf16[256,2,2048]{0,2,1:T(8,128)(2,1)}, f32[256,2,2048]{0,2,1:T(8,128)}, f32[256,2,2048]{0,2,1:T(8,128)}, f32[256,2,2048]{0,2,1:T(8,128)}) fusion(f32[256,2,2048]{0,2,1:T(8,128)} %copy.13, f32[256,2,2048]{0,2,1:T(8,128)} %reduce-scatter.2.cloned.1.call-done, f32[]{:T(128)S(6)} %div.18, f32[256,2,2048]{0,2,1:T(8,128)} %copy.9, f32[256,2,2048]{0,2,1:T(8,128)} %copy.11), kind=kLoop, calls=%fused_computation.6 | loop fusion | flops 17825792 | bytes 31457284 | tf_op jit(solution)/shard_map/convert_element_type | solution.py:50
  422.7 0.0 all-gather.2.cloned.1.call-update
  422.7 7.3 %copy.14 = f32[256,2,2048]{2,1,0:T(2,128)} copy(f32[256,2,2048]{0,2,1:T(8,128)} %get-tuple-element.9) | data formatting | bytes 8388608
  430.0 7.7 %copy.15 = f32[256,2,2048]{2,1,0:T(2,128)} copy(f32[256,2,2048]{0,2,1:T(8,128)} %get-tuple-element.10) | data formatting | bytes 8388608
  437.7 7.3 %copy.16 = f32[256,2,2048]{2,1,0:T(2,128)} copy(f32[256,2,2048]{0,2,1:T(8,128)} %get-tuple-element.11) | data formatting | bytes 8388608
  445.0 130.3 %all-gather.2.cloned.1.call-done = bf16[2048,2,2048]{0,2,1:T(8,128)(2,1)} async-done(((bf16[256,2,2048]{0,2,1:T(8,128)(2,1)}), bf16[2048,2,2048]{0,2,1:T(8,128)(2,1)}) %all-gather.2.cloned.1.call-update) | async-done | bytes 16777232 | tf_op jit(solution)/shard_map/all_gather | solution.py:51
  575.3 41.5 %copy.17 = bf16[2048,2,2048]{2,1,0:T(2,128)(2,1)} copy(bf16[2048,2,2048]{0,2,1:T(8,128)(2,1)} %all-gather.2.cloned.1.call-done) | data formatting | bytes 33554432
Async XLA Ops:
  7.2 354.1 %reduce-scatter.2.cloned.1.call-start = ((), (), s32[]{:S(2)}) async-start(), calls=%async_computation.1 | async-start | bytes 37748736 | tf_op jit(solution)/shard_map/reduce_scatter | solution.py:19
  32.9 542.4 %all-gather.2.cloned.1.call-start = ((), (), s32[]{:S(2)}) async-start(), calls=%async_computation.2 | async-start | bytes 18874368 | tf_op jit(solution)/shard_map/all_gather | solution.py:51
Sparse Core Ops, SparseCore 0:
  33.0 328.1 reduce-scatter.1
  422.8 152.4 all-gather.1
where the time goes:
time: 626 us; the launch traced here: 624 us
  waiting for transfers between devices  444 us (71%)
  local copies, waits for them, and re-layouts  85.4 us (14%)
  blocking collectives  37.9 us (6%)
  matrix products  25.6 us (4%)
  other arithmetic  15.6 us (2%)
  between operations  14.8 us (2%)
    reduce_scatter x1, waiting for transfers between devices, reduce_rows(): lax.psum_scatter(jnp.einsum('ltr,ltc->rlc', layer_acts, layer_grads, pref...  314 us
    all_gather x1, waiting for transfers between devices, on_device(): tp_rows = lax.all_gather(rounded, 'dp', axis=0, tiled=True)  130 us
    unnamed x7, local copies, waits for them, and re-layouts  85.4 us
    psum x1, blocking collectives, on_device(): sum_squares = lax.psum(layer_sum, ('tp', 'dp'))  37.9 us
    dot_general x1, matrix products, reduce_rows(): jnp.einsum('ltr,ltc->rlc', layer_acts, layer_grads, preferred_element_typ...  25.6 us
  transfers between devices with their start and end apart: 2, of which 2 were waited for; matrix products, arithmetic and copies ran while one was open for 6% of the time, Pallas kernels for 0%

commit v1 on v0

--- a/solution.py
+++ b/solution.py
@@ -1,8 +1,12 @@
+import functools
 import math
 
 import jax
 import jax.numpy as jnp
 from jax import lax
+from jax.experimental import pallas as pl
+from jax.experimental.layout import Layout, with_layout_constraint
+from jax.experimental.pallas import tpu as pltpu
 from jax.sharding import PartitionSpec as P
 
 beta_first = 0.9
@@ -13,17 +17,124 @@
 decay_rate = 0.1
 epsilon = 1e-08
 limit_scale = 2.0
+MESH = pl.DeviceIdType.MESH
 
 
-def reduce_rows(layer_acts, layer_grads):
-    grad_own = lax.psum_scatter(
-        jnp.einsum("ltr,ltc->rlc", layer_acts, layer_grads, preferred_element_type=jnp.float32),
-        "dp",
-        scatter_dimension=0,
-        tiled=True,
-    )
-    partial_value = jnp.sum(grad_own * grad_own)
-    return (grad_own, partial_value)
+def total_kernel(n_tp, n_dp, value_ref, total_ref, held, send_sem, recv_sem):
+    count = n_tp * n_dp
+    me = lax.axis_index("tp") * n_dp + lax.axis_index("dp")
+
+    def device(k):
+        other = lax.rem(me + k, count)
+        return {"tp": other // n_dp, "dp": lax.rem(other, n_dp)}
+
+    def copy(k, slot):
+        return pltpu.make_async_remote_copy(
+            src_ref=value_ref,
+            dst_ref=held.at[slot],
+            send_sem=send_sem.at[k],
+            recv_sem=recv_sem.at[k],
+            device_id=device(k),
+            device_id_type=MESH,
+        )
+
+    barrier = pltpu.get_barrier_semaphore()
+
+    @pl.loop(1, count)
+    def _(k):
+        pl.semaphore_signal(barrier, inc=1, device_id=device(k), device_id_type=MESH)
+
+    pl.semaphore_wait(barrier, count - 1)
+
+    @pl.loop(1, count)
+    def _(k):
+        copy(k, me).start()
+
+    held[me] = value_ref[...]
+
+    @pl.loop(1, count)
+    def _(k):
+        copy(k, lax.rem(me - k + count, count)).wait()
+
+    total_ref[...] = jnp.sum(held[...], axis=0)
+
+
+def device_total(value):
+    n_tp, n_dp = lax.axis_size("tp"), lax.axis_size("dp")
+    count = n_tp * n_dp
+    total = pl.pallas_call(
+        functools.partial(total_kernel, n_tp, n_dp),
+        out_shape=jax.ShapeDtypeStruct((8, 128), jnp.float32),
+        in_specs=[pl.BlockSpec(memory_space=pltpu.VMEM)],
+        out_specs=pl.BlockSpec(memory_space=pltpu.VMEM),
+        scratch_shapes=[
+            pltpu.VMEM((count, 8, 128), jnp.float32),
+            pltpu.SemaphoreType.DMA((count,)),
+            pltpu.SemaphoreType.DMA((count,)),
+        ],
+        compiler_params=pltpu.CompilerParams(collective_id=0, has_side_effects=True),
+        name="device_total",
+    )(jnp.full((8, 128), value, jnp.float32))
+    return total[0, 0]
+
+
+def reduce_rows(activations, out_grads):
+    n_dp = lax.axis_size("dp")
+    cores = 2 if n_dp % 2 == 0 else 1
+    chips = n_dp // cores
+    index = lax.axis_index("dp")
+    chip, core = index // cores, lax.rem(index, cores)
+    layers, tokens, width = activations.shape
+    rows = width // n_dp
+    top = jnp.max(jnp.abs(activations)).astype(jnp.float32)
+    top = top * jnp.max(jnp.abs(out_grads)).astype(jnp.float32)
+    bound = jnp.maximum(device_total(tokens * top), 1e-25)
+    shrink, grow = 32000.0 / bound, bound / 32000.0
+
+    def pack(x):
+        return (x * shrink).astype(jnp.float16)
+
+    def unpack(x):
+        return x.astype(jnp.float32) * grow
+
+    swap = [(i, i // cores * cores + (i + 1) % cores) for i in range(n_dp)]
+    owns, outs = [], []
+    split = activations.reshape(layers, tokens, chips, cores, rows)
+
+    def product(layer, which):
+        acts = lax.dynamic_index_in_dim(split[layer], which, 2, keepdims=False)
+        acts = acts.reshape(tokens, chips * rows)
+        return jnp.einsum("tr,tc->rc", acts, out_grads[layer], preferred_element_type=jnp.float32)
+
+    for layer in range(layers):
+        if cores == 2:
+            sent = lax.ppermute(pack(product(layer, 1 - core)), "dp", swap)
+            outs.append(sent.reshape(chips, rows, -1))
+        owns.append(product(layer, core).reshape(chips, rows, -1))
+
+    def block(layer, which):
+        value = lax.dynamic_index_in_dim(owns[layer], which, 0, keepdims=False)
+        if cores == 2:
+            value = value + unpack(lax.dynamic_index_in_dim(outs[layer], which, 0, keepdims=False))
+        return value
+
+    running = [None] * layers
+    for step in range(chips - 1):
+        for layer in range(layers):
+            way = 1 if layer % 2 == 0 else -1
+            which = lax.rem(chip - way * (1 + step) + chips, chips)
+            value = block(layer, which)
+            if running[layer] is not None:
+                value = value + unpack(running[layer])
+            ring = [(i, (i + way * cores) % n_dp) for i in range(n_dp)]
+            running[layer] = lax.ppermute(pack(value), "dp", ring)
+    done = []
+    for layer in range(layers):
+        value = block(layer, chip)
+        if running[layer] is not None:
+            value = value + unpack(running[layer])
+        done.append(value)
+    return done
 
 
 def adam_update(grad_own, master, first_moment, second_moment, clip_factor):
@@ -37,13 +148,14 @@
 
 def on_device(activations, out_grads, master, first_moment, second_moment):
     own_rows = master.shape[0]
-    grad_own, layer_sum = reduce_rows(activations, out_grads)
-    sum_squares = lax.psum(layer_sum, ("tp", "dp"))
+    layer_grads = reduce_rows(activations, out_grads)
+    sum_squares = device_total(sum(jnp.sum(g * g) for g in layer_grads))
     entries = (
         own_rows * lax.axis_size("tp") * lax.axis_size("dp") * master.shape[1] * master.shape[2]
     )
     limit = limit_scale * math.sqrt(entries)
     clip_factor = limit / jnp.maximum(jnp.sqrt(sum_squares), limit)
+    grad_own = with_layout_constraint(jnp.stack(layer_grads, axis=1), Layout((0, 1, 2)))
     new_master, new_first, new_second = adam_update(
         grad_own, master, first_moment, second_moment, clip_factor
     )

time: 626 us -> 439 us (0.70)
  waiting for transfers between devices: 444 us -> 249 us
  blocking collectives: 37.9 us -> 0 us
  other arithmetic: 15.6 us -> 53.1 us
  local copies, waits for them, and re-layouts: 85.4 us -> 48.6 us
  Pallas kernels: 0 us -> 24.3 us
  starting transfers between devices: 0.08 us -> 14.5 us
    reduce_scatter x1 -> x0, waiting for transfers between devices: 314 us -> none  [reduce_rows(): lax.psum_scatter(jnp.einsum('ltr,ltc->rlc', layer_acts, layer_grads, pref...]
    ppermute x0 -> x8, waiting for transfers between devices: none -> 97.4 us  [the longest x6 97.4 us: reduce_rows(): running[layer] = lax.ppermute(pack(value), 'dp', ring)]
    unnamed x7 -> x11, local copies, waits for them, and re-layouts: 85.4 us -> 31.2 us
    psum x1 -> x0, blocking collectives: 37.9 us -> none  [on_device(): sum_squares = lax.psum(layer_sum, ('tp', 'dp'))]
    pallas_call x0 -> x2, Pallas kernels: none -> 24.3 us  [device_total(): pl.pallas_call(functools.partial(total_kernel, n_tp, n_dp), out_shape=jax...]
    all_gather x1, waiting for transfers between devices: 130 us -> 151 us  [on_device(): tp_rows = lax.all_gather(rounded, 'dp', axis=0, tiled=True)]
    ppermute x0 -> x8, starting transfers between devices: none -> 14.5 us  [the longest x6 14 us: reduce_rows(): running[layer] = lax.ppermute(pack(value), 'dp', ring)]
    convert_element_type x0 -> x4, other arithmetic: none -> 11.5 us  [pack(): return (x * shrink).astype(jnp.float16)]
  transfers between devices with their start and end apart: 2 -> 9, of which waited for: 2 -> 7; matrix products, arithmetic and copies ran while one was open for 6% -> 10% of each run, Pallas kernels for 0% -> 0%
where the time goes in v1:
time: 439 us; the launch traced here: 438 us
  waiting for transfers between devices  249 us (57%)
  other arithmetic  53.1 us (12%)
  local copies, waits for them, and re-layouts  48.6 us (11%)
  matrix products  30.3 us (7%)
  Pallas kernels  24.3 us (6%)
  between operations  18.2 us (4%)
  starting transfers between devices  14.5 us (3%)
    all_gather x1, waiting for transfers between devices, on_device(): tp_rows = lax.all_gather(rounded, 'dp', axis=0, tiled=True)  151 us
    ppermute x6, waiting for transfers between devices, reduce_rows(): running[layer] = lax.ppermute(pack(value), 'dp', ring)  97.4 us
    unnamed x11, local copies, waits for them, and re-layouts  31.2 us
    dot_general x4, matrix products, product(): jnp.einsum('tr,tc->rc', acts, out_grads[layer], preferred_element_type=jn...  30.3 us
    pallas_call x2, Pallas kernels, device_total(): pl.pallas_call(functools.partial(total_kernel, n_tp, n_dp), out_shape=jax...  24.3 us
    convert_element_type x1, other arithmetic, on_device(): rounded = new_master.astype(jnp.bfloat16)  20.7 us
    ppermute x6, starting transfers between devices, reduce_rows(): running[layer] = lax.ppermute(pack(value), 'dp', ring)  14 us
    convert_element_type x4, other arithmetic, pack(): return (x * shrink).astype(jnp.float16)  11.5 us
  transfers between devices with their start and end apart: 9, of which 7 were waited for; matrix products, arithmetic and copies ran while one was open for 10% of the time, Pallas kernels for 0%

profile of v1, /device:TPU:0, one launch (start us, length us, event | category | flops | bytes accessed | tf_op | source)
XLA Modules:
  0.0 437.9 jit_solution(4437130009066373537)
XLA Ops:
  7.2 6.1 %fusion.30 = (bf16[1,1024,2048]{2,1,0:T(8,128)(2,1)}, bf16[1,1024,2048]{2,1,0:T(8,128)(2,1)}) fusion(bf16[2,1024,2048]{2,1,0:T(8,128)(2,1)} %param.5), kind=kLoop, calls=%fused_computation.49 | loop fusion | bytes 16777216 | tf_op jit(solution)/shard_map/slice | solution.py:105
  13.4 10.4 %abs_reduce_fusion = (bf16[]{:T(256)}, bf16[]{:T(256)}) fusion(bf16[2,1024,2048]{2,1,0:T(8,128)(2,1)} %param.6, bf16[2,1024,2048]{2,1,0:T(8,128)(2,1)} %param.5), kind=kLoop, calls=%fused_computation.2 | loop fusion | flops 16777214 | bytes 16777220 | tf_op jit(solution)/shard_map/reduce_max | solution.py:90
  25.7 13.1 %device_total.2 = f32[8,128]{1,0:T(8,128)} custom-call(f32[8,128]{1,0:T(8,128)} %broadcast_in_dim.6.value_ref), custom_call_target="tpu_custom_call" | custom-call | tf_op jit(solution)/shard_map/device_total/pallas_call | solution.py:65
  40.0 6.4 %copy.23 = bf16[1,1024,2048]{1,2,0:T(8,128)(2,1)} copy(bf16[1,1024,2048]{2,1,0:T(8,128)(2,1)} %get-tuple-element.12) | data formatting | bytes 8388608
  46.3 6.4 %copy.24 = bf16[1,1024,2048]{1,2,0:T(8,128)(2,1)} copy(bf16[1,1024,2048]{2,1,0:T(8,128)(2,1)} %get-tuple-element.13) | data formatting | bytes 8388608
  53.4 2.8 constant_dynamic-slice_fusion
  56.3 8.4 %multiply_convert_fusion = f16[1024,2048]{1,0:T(8,128)(2,1)} fusion(bf16[1024,1024]{0,1:T(8,128)(2,1)S(1)} %bitcast.83, f32[]{:T(128)} %bitcast.7, bf16[2,1024,2048]{2,1,0:T(8,128)(2,1)} %param.6), kind=kOutput, calls=%fused_computation | convolution fusion | flops 4299161600 | bytes 10486272 | tf_op jit(solution)/shard_map/tr,tc->rc/dot_general | solution.py:107
  64.8 6.1 %multiply_convert_fusion.1 = f16[1024,2048]{1,0:T(8,128)(2,1)} fusion(bf16[1024,1024]{0,1:T(8,128)(2,1)S(1)} %bitcast.82, f32[]{:T(128)} %bitcast.7, bf16[2,1024,2048]{2,1,0:T(8,128)(2,1)S(1)} %bitcast.81), kind=kOutput, calls=%fused_computation.1 | convolution fusion | flops 4299161600 | bytes 10485764 | tf_op jit(solution)/shard_map/tr,tc->rc/dot_general | solution.py:107
  71.3 6.9 %fusion.1 = f32[4,256,2048]{2,1,0:T(8,128)S(1)} fusion(bf16[2,1024,2048]{2,1,0:T(8,128)(2,1)} %param.6, bf16[1024,4,2,256]{0,3,2,1:T(8,128)(2,1)} %bitcast.79, s32[]{:T(128)S(6)} %select_n.46), kind=kOutput, calls=%fused_computation.7 | convolution fusion | flops 4294967296 | bytes 14680068 | tf_op jit(solution)/shard_map/tr,tc->rc/dot_general | solution.py:107
  78.3 4.2 copy-done.1
  84.2 2.9 collective-permute-start.5
  87.1 8.9 %fusion.4 = f32[4,256,2048]{2,1,0:T(8,128)} fusion(bf16[2,1024,2048]{2,1,0:T(8,128)(2,1)} %param.6, bf16[1024,4,2,256]{0,3,2,1:T(8,128)(2,1)S(1)} %bitcast.77, s32[]{:T(128)S(6)} %select_n.46), kind=kOutput, calls=%fused_computation.10 | convolution fusion | flops 4294967296 | bytes 14680068 | tf_op jit(solution)/shard_map/tr,tc->rc/dot_general | solution.py:107
  96.0 2.2 fusion.23
  98.4 12.3 %collective-permute-done.5 = f16[256,2048]{1,0:T(8,128)(2,1)S(1)} collective-permute-done((f16[256,2048]{1,0:T(8,128)(2,1)S(1)}, f16[256,2048]{1,0:T(8,128)(2,1)S(1)}, u32[]{:S(2)}, u32[]{:S(2)}) %collective-permute-start.5) | collective-permute-done | bytes 1048608 | tf_op jit(solution)/shard_map/ppermute | solution.py:130
  110.7 2.5 fusion.14
  113.2 4.3 collective-permute-start.6
  117.5 16.7 %collective-permute-done.1 = f16[256,2048]{1,0:T(8,128)(2,1)} collective-permute-done((f16[256,2048]{1,0:T(8,128)(2,1)S(1)}, f16[256,2048]{1,0:T(8,128)(2,1)}, u32[]{:S(2)}, u32[]{:S(2)}) %collective-permute-start.1) | collective-permute-done | bytes 1048608 | tf_op jit(solution)/shard_map/ppermute | solution.py:130
  134.2 2.8 fusion.18
  138.6 18.0 %collective-permute-done.6 = f16[256,2048]{1,0:T(8,128)(2,1)} collective-permute-done((f16[256,2048]{1,0:T(8,128)(2,1)S(1)}, f16[256,2048]{1,0:T(8,128)(2,1)}, u32[]{:S(2)}, u32[]{:S(2)}) %collective-permute-start.6) | collective-permute-done | bytes 1048608 | tf_op jit(solution)/shard_map/ppermute | solution.py:130
  156.6 2.8 fusion.16
  159.4 3.5 collective-permute-start.7
  162.9 16.2 %collective-permute-done.2 = f16[256,2048]{1,0:T(8,128)(2,1)S(1)} collective-permute-done((f16[256,2048]{1,0:T(8,128)(2,1)S(1)}, f16[256,2048]{1,0:T(8,128)(2,1)S(1)}, u32[]{:S(2)}, u32[]{:S(2)}) %collective-permute-start.2) | collective-permute-done | bytes 1048608 | tf_op jit(solution)/shard_map/ppermute | solution.py:130
  179.1 3.4 fusion.20
  184.1 17.5 %collective-permute-done.7 = f16[256,2048]{1,0:T(8,128)(2,1)} collective-permute-done((f16[256,2048]{1,0:T(8,128)(2,1)S(1)}, f16[256,2048]{1,0:T(8,128)(2,1)}, u32[]{:S(2)}, u32[]{:S(2)}) %collective-permute-start.7) | collective-permute-done | bytes 1048608 | tf_op jit(solution)/shard_map/ppermute | solution.py:130
  201.6 3.4 multiply_reduce_fusion
  206.4 16.7 %collective-permute-done.3 = f16[256,2048]{1,0:T(8,128)(2,1)S(1)} collective-permute-done((f16[256,2048]{1,0:T(8,128)(2,1)}, f16[256,2048]{1,0:T(8,128)(2,1)S(1)}, u32[]{:S(2)}, u32[]{:S(2)}) %collective-permute-start.3) | collective-permute-done | bytes 1048608 | tf_op jit(solution)/shard_map/ppermute | solution.py:130
  223.2 3.1 multiply_reduce_fusion.1
  226.2 3.5 copy.22
  231.6 11.2 %device_total.3 = f32[8,128]{1,0:T(8,128)} custom-call(f32[8,128]{1,0:T(8,128)} %broadcast_in_dim.7.value_ref), custom_call_target="tpu_custom_call" | custom-call | tf_op jit(solution)/shard_map/device_total/pallas_call | solution.py:65
  244.8 20.7 %fusion.28 = (bf16[256,2,2048]{2,1,0:T(2,128)(2,1)}, f32[256,2,2048]{2,1,0:T(2,128)}, f32[256,2,2048]{2,1,0:T(2,128)}, f32[256,2,2048]{2,1,0:T(2,128)}) fusion(f32[256,2,2048]{2,1,0:T(2,128)} %param.7, f32[256,1,2048]{2,1,0:T(1,128)S(1)} %stack.10, f32[256,1,2048]{2,1,0:T(1,128)} %copy.22, f32[]{:T(128)} %bitcast.26, f32[256,2,2048]{2,1,0:T(2,128)} %param.8, ...), kind=kLoop, calls=%fused_computation.48 | loop fusion | flops 18874368 | bytes 31457284 | tf_op jit(solution)/shard_map/convert_element_type | solution.py:162
  265.5 151.4 %all-gather.2.cloned.1.call-done = bf16[2048,2,2048]{2,1,0:T(2,128)(2,1)} async-done(((bf16[256,2,2048]{2,1,0:T(2,128)(2,1)}), bf16[2048,2,2048]{2,1,0:T(2,128)(2,1)}) %all-gather.2.cloned.1.call-update) | async-done | bytes 16777232 | tf_op jit(solution)/shard_map/all_gather | solution.py:163
  416.9 14.1 %copy.26 = bf16[2048,2,2048]{2,1,0:T(2,128)(2,1)} copy(bf16[2048,2,2048]{2,1,0:T(2,128)(2,1)} %all-gather.2.cloned.1.call-done) | data formatting | bytes 33554432
  (23 shorter events, 10.5 us)
Async XLA Ops:
  7.2 409.8 %all-gather.2.cloned.1.call-start = ((), (), s32[]{:S(2)}) async-start(), calls=%async_computation | async-start | bytes 18874368 | tf_op jit(solution)/shard_map/all_gather | solution.py:163
  53.4 11.4 %slice-start = ((s8[8388608]{0:T(1024)(128)(4,1)}), s8[4194304]{0:T(1024)(128)(4,1)S(1)}, s32[]{:S(2)}) async-start(s8[8388608]{0:T(1024)(128)(4,1)} %bitcast.80), calls=%async_computation.1 | async-start | bytes 8388608
  56.3 8.5 %slice-start.1 = ((s8[8388608]{0:T(1024)(128)(4,1)}), s8[4194304]{0:T(1024)(128)(4,1)S(1)}, s32[]{:S(2)}) async-start(s8[8388608]{0:T(1024)(128)(4,1)} %bitcast.80), calls=%async_computation.2 | async-start | bytes 8388608
  64.7 13.6 %collective-permute-start.4 = (f16[1024,2048]{1,0:T(8,128)(2,1)}, f16[1024,2048]{1,0:T(8,128)(2,1)}, u32[]{:S(2)}, u32[]{:S(2)}) collective-permute-start(f16[1024,2048]{1,0:T(8,128)(2,1)} %multiply_convert_fusion), channel_id=1, source_target_pairs={{0,1},{1,0},{2,3},{3,2},{4,5},{5,4},{6,7},{7,6},{8,9},{9,8},{10,11... | collective-permute-start | bytes 12582920 | tf_op jit(solution)/shard_map/ppermute | solution.py:111
  70.9 25.1 %collective-permute-start = (f16[1024,2048]{1,0:T(8,128)(2,1)}, f16[1024,2048]{1,0:T(8,128)(2,1)}, u32[]{:S(2)}, u32[]{:S(2)}) collective-permute-start(f16[1024,2048]{1,0:T(8,128)(2,1)} %multiply_convert_fusion.1), channel_id=1, source_target_pairs={{0,1},{1,0},{2,3},{3,2},{4,5},{5,4},{6,7},{7,6},{8,9},{9,8},{10,11... | collective-permute-start | bytes 12582920 | tf_op jit(solution)/shard_map/ppermute | solution.py:111
  78.2 4.3 copy-start.1
  78.2 8.8 %copy-start = (bf16[1,1024,2048]{1,2,0:T(8,128)(2,1)S(1)}, bf16[1,1024,2048]{1,2,0:T(8,128)(2,1)}, u32[]{:S(2)}) copy-start(bf16[1,1024,2048]{1,2,0:T(8,128)(2,1)} %copy.23) | copy-start | bytes 12582916
  84.2 26.5 %collective-permute-start.5 = (f16[256,2048]{1,0:T(8,128)(2,1)S(1)}, f16[256,2048]{1,0:T(8,128)(2,1)S(1)}, u32[]{:S(2)}, u32[]{:S(2)}) collective-permute-start(f16[256,2048]{1,0:T(8,128)(2,1)S(1)} %fusion.24), channel_id=1, source_target_pairs={{0,6},{1,7},{2,0},{3,1},{4,2},{5,3},{6,4},{7,5},{8,14},{9,15},{10,... | collective-permute-start | bytes 3145736 | tf_op jit(solution)/shard_map/ppermute | solution.py:130
  98.3 35.9 %collective-permute-start.1 = (f16[256,2048]{1,0:T(8,128)(2,1)S(1)}, f16[256,2048]{1,0:T(8,128)(2,1)}, u32[]{:S(2)}, u32[]{:S(2)}) collective-permute-start(f16[256,2048]{1,0:T(8,128)(2,1)S(1)} %fusion.23), channel_id=1, source_target_pairs={{0,2},{1,3},{2,4},{3,5},{4,6},{5,7},{6,0},{7,1},{8,10},{9,11},{10,... | collective-permute-start | bytes 3145736 | tf_op jit(solution)/shard_map/ppermute | solution.py:130
  113.2 43.4 %collective-permute-start.6 = (f16[256,2048]{1,0:T(8,128)(2,1)S(1)}, f16[256,2048]{1,0:T(8,128)(2,1)}, u32[]{:S(2)}, u32[]{:S(2)}) collective-permute-start(f16[256,2048]{1,0:T(8,128)(2,1)S(1)} %fusion.14), channel_id=1, source_target_pairs={{0,6},{1,7},{2,0},{3,1},{4,2},{5,3},{6,4},{7,5},{8,14},{9,15},{10,... | collective-permute-start | bytes 3145736 | tf_op jit(solution)/shard_map/ppermute | solution.py:130
  137.0 42.1 %collective-permute-start.2 = (f16[256,2048]{1,0:T(8,128)(2,1)S(1)}, f16[256,2048]{1,0:T(8,128)(2,1)S(1)}, u32[]{:S(2)}, u32[]{:S(2)}) collective-permute-start(f16[256,2048]{1,0:T(8,128)(2,1)S(1)} %fusion.18), channel_id=1, source_target_pairs={{0,2},{1,3},{2,4},{3,5},{4,6},{5,7},{6,0},{7,1},{8,10},{9,11},{10,... | collective-permute-start | bytes 3145736 | tf_op jit(solution)/shard_map/ppermute | solution.py:130
  159.4 42.2 %collective-permute-start.7 = (f16[256,2048]{1,0:T(8,128)(2,1)S(1)}, f16[256,2048]{1,0:T(8,128)(2,1)}, u32[]{:S(2)}, u32[]{:S(2)}) collective-permute-start(f16[256,2048]{1,0:T(8,128)(2,1)S(1)} %fusion.16), channel_id=1, source_target_pairs={{0,6},{1,7},{2,0},{3,1},{4,2},{5,3},{6,4},{7,5},{8,14},{9,15},{10,... | collective-permute-start | bytes 3145736 | tf_op jit(solution)/shard_map/ppermute | solution.py:130
  182.5 40.7 %collective-permute-start.3 = (f16[256,2048]{1,0:T(8,128)(2,1)}, f16[256,2048]{1,0:T(8,128)(2,1)S(1)}, u32[]{:S(2)}, u32[]{:S(2)}) collective-permute-start(f16[256,2048]{1,0:T(8,128)(2,1)} %fusion.20), channel_id=1, source_target_pairs={{0,2},{1,3},{2,4},{3,5},{4,6},{5,7},{6,0},{7,1},{8,10},{9,11},{10,... | collective-permute-start | bytes 3145736 | tf_op jit(solution)/shard_map/ppermute | solution.py:130
Sparse Core Ops, SparseCore 0:
  265.6 151.2 all-gather.1

commit v2 on v1

--- a/solution.py
+++ b/solution.py
@@ -56,7 +56,8 @@
     def _(k):
         copy(k, lax.rem(me - k + count, count)).wait()
 
-    total_ref[...] = jnp.sum(held[...], axis=0)
+    total_ref[0] = jnp.sum(held[...], axis=0)
+    total_ref[1] = jnp.sum(held[pl.ds(lax.axis_index("tp") * n_dp, n_dp)], axis=0)
 
 
 def device_total(value):
@@ -64,7 +65,7 @@
     count = n_tp * n_dp
     total = pl.pallas_call(
         functools.partial(total_kernel, n_tp, n_dp),
-        out_shape=jax.ShapeDtypeStruct((8, 128), jnp.float32),
+        out_shape=jax.ShapeDtypeStruct((2, 8, 128), jnp.float32),
         in_specs=[pl.BlockSpec(memory_space=pltpu.VMEM)],
         out_specs=pl.BlockSpec(memory_space=pltpu.VMEM),
         scratch_shapes=[
@@ -75,7 +76,7 @@
         compiler_params=pltpu.CompilerParams(collective_id=0, has_side_effects=True),
         name="device_total",
     )(jnp.full((8, 128), value, jnp.float32))
-    return total[0, 0]
+    return total[0, 0, 0], total[1, 0, 0]
 
 
 def reduce_rows(activations, out_grads):
@@ -86,55 +87,53 @@
     chip, core = index // cores, lax.rem(index, cores)
     layers, tokens, width = activations.shape
     rows = width // n_dp
-    top = jnp.max(jnp.abs(activations)).astype(jnp.float32)
-    top = top * jnp.max(jnp.abs(out_grads)).astype(jnp.float32)
-    bound = jnp.maximum(device_total(tokens * top), 1e-25)
-    shrink, grow = 32000.0 / bound, bound / 32000.0
+
+    def longest(x):
+        squares = jnp.sum(jnp.square(x.astype(jnp.float32)), axis=1)
+        return jnp.sqrt(jnp.max(squares))
+
+    _, bound = device_total(longest(activations) * longest(out_grads))
+    bound = jnp.maximum(1.001 * bound, 1e-25)
+    shrink, grow = 250.0 / bound, bound / 250.0
 
     def pack(x):
-        return (x * shrink).astype(jnp.float16)
+        x = x * shrink
+        return (x * jnp.abs(x)).astype(jnp.float16)
 
     def unpack(x):
-        return x.astype(jnp.float32) * grow
+        x = x.astype(jnp.float32)
+        return jnp.sign(x) * jnp.sqrt(jnp.abs(x)) * grow
 
     swap = [(i, i // cores * cores + (i + 1) % cores) for i in range(n_dp)]
-    owns, outs = [], []
-    split = activations.reshape(layers, tokens, chips, cores, rows)
+    ways = [1 if layer % 2 == 0 else -1 for layer in range(layers)]
+    rings = [[(i, (i + way * cores) % n_dp) for i in range(n_dp)] for way in ways]
 
-    def product(layer, which):
-        acts = lax.dynamic_index_in_dim(split[layer], which, 2, keepdims=False)
-        acts = acts.reshape(tokens, chips * rows)
+    def product(acts, layer, which, half):
+        start = (which * cores + half) * rows
+        acts = lax.dynamic_slice_in_dim(acts[layer], start, rows, axis=1)
         return jnp.einsum("tr,tc->rc", acts, out_grads[layer], preferred_element_type=jnp.float32)
 
-    for layer in range(layers):
-        if cores == 2:
-            sent = lax.ppermute(pack(product(layer, 1 - core)), "dp", swap)
-            outs.append(sent.reshape(chips, rows, -1))
-        owns.append(product(layer, core).reshape(chips, rows, -1))
+    def block(acts, layer, step):
+        which = lax.rem(chip - ways[layer] * (1 + step) + 2 * chips, chips)
+        if cores == 1:
+            return product(acts, layer, which, core)
+        other = lax.ppermute(pack(product(acts, layer, which, 1 - core)), "dp", swap)
+        return product(acts, layer, which, core) + unpack(other)
 
-    def block(layer, which):
-        value = lax.dynamic_index_in_dim(owns[layer], which, 0, keepdims=False)
-        if cores == 2:
-            value = value + unpack(lax.dynamic_index_in_dim(outs[layer], which, 0, keepdims=False))
-        return value
-
-    running = [None] * layers
-    for step in range(chips - 1):
-        for layer in range(layers):
-            way = 1 if layer % 2 == 0 else -1
-            which = lax.rem(chip - way * (1 + step) + chips, chips)
-            value = block(layer, which)
-            if running[layer] is not None:
-                value = value + unpack(running[layer])
-            ring = [(i, (i + way * cores) % n_dp) for i in range(n_dp)]
-            running[layer] = lax.ppermute(pack(value), "dp", ring)
-    done = []
-    for layer in range(layers):
-        value = block(layer, chip)
-        if running[layer] is not None:
-            value = value + unpack(running[layer])
-        done.append(value)
-    return done
+    values = [block(activations, layer, 0) for layer in range(layers)]
+    if chips > 1:
+        first = [pack(value) for value in values]
+        activations, first = lax.optimization_barrier((activations, first))
+        later = [
+            [block(activations, layer, step) for layer in range(layers)]
+            for step in range(1, chips)
+        ]
+        running = [lax.ppermute(first[i], "dp", rings[i]) for i in range(layers)]
+        for step, blocks in enumerate(later, 1):
+            values = [blocks[i] + unpack(running[i]) for i in range(layers)]
+            if step < chips - 1:
+                running = [lax.ppermute(pack(values[i]), "dp", rings[i]) for i in range(layers)]
+    return values
 
 
 def adam_update(grad_own, master, first_moment, second_moment, clip_factor):
@@ -149,7 +148,7 @@
 def on_device(activations, out_grads, master, first_moment, second_moment):
     own_rows = master.shape[0]
     layer_grads = reduce_rows(activations, out_grads)
-    sum_squares = device_total(sum(jnp.sum(g * g) for g in layer_grads))
+    sum_squares, _ = device_total(sum(jnp.sum(g * g) for g in layer_grads))
     entries = (
         own_rows * lax.axis_size("tp") * lax.axis_size("dp") * master.shape[1] * master.shape[2]
     )

time: 439 us -> 431 us (0.982)
  local copies, waits for them, and re-layouts: 48.6 us -> 28.2 us
    unnamed x11, local copies, waits for them, and re-layouts: 31.2 us -> 14.2 us
    reduce_sum x2 -> x4, other arithmetic: 6.51 us -> 17.9 us  [the longest x2 11.3 us: longest(): squares = jnp.sum(jnp.square(x.astype(jnp.float32)), axis=1)]
    reduce_max x1 -> x2, other arithmetic: 10.4 us -> 1.23 us  [longest(): return jnp.sqrt(jnp.max(squares))]
    dot_general x4 -> x16, matrix products: 30.3 us -> 34.5 us  [product(): jnp.einsum('tr,tc->rc', acts, out_grads[layer], preferred_element_type=jn...]
    ppermute x8 -> x14, starting transfers between devices: 14.5 us -> 17 us  [the longest x4 11.4 us: reduce_rows(): lax.ppermute(pack(values[i]), 'dp', rings[i])]
    ppermute x8 -> x14, waiting for transfers between devices: 97.4 us -> 98.5 us  [the longest x4 70.5 us: reduce_rows(): lax.ppermute(pack(values[i]), 'dp', rings[i])]
  transfers between devices with their start and end apart: 9 -> 15, of which waited for: 7 -> 7; matrix products, arithmetic and copies ran while one was open for 10% -> 10% of each run, Pallas kernels for 0% -> 0%
where the time goes in v2:
time: 431 us; the launch traced here: 428 us
  waiting for transfers between devices  250 us (58%)
  other arithmetic  51.5 us (12%)
  matrix products  34.5 us (8%)
  Pallas kernels  28.5 us (7%)
  local copies, waits for them, and re-layouts  28.2 us (7%)
  between operations  18.6 us (4%)
  starting transfers between devices  17.1 us (4%)
    all_gather x1, waiting for transfers between devices, on_device(): tp_rows = lax.all_gather(rounded, 'dp', axis=0, tiled=True)  151 us
    ppermute x4, waiting for transfers between devices, reduce_rows(): lax.ppermute(pack(values[i]), 'dp', rings[i])  70.5 us
    dot_general x16, matrix products, product(): jnp.einsum('tr,tc->rc', acts, out_grads[layer], preferred_element_type=jn...  34.5 us
    pallas_call x2, Pallas kernels, device_total(): pl.pallas_call(functools.partial(total_kernel, n_tp, n_dp), out_shape=jax...  28.5 us
    ppermute x2, waiting for transfers between devices, reduce_rows(): running = [lax.ppermute(first[i], 'dp', rings[i]) for i in range(layers)]  28 us
    convert_element_type x1, other arithmetic, on_device(): rounded = new_master.astype(jnp.bfloat16)  20.8 us
    unnamed x11, local copies, waits for them, and re-layouts  14.2 us
    convert_element_type x4, other arithmetic, pack(): return (x * jnp.abs(x)).astype(jnp.float16)  11.5 us
  transfers between devices with their start and end apart: 15, of which 7 were waited for; matrix products, arithmetic and copies ran while one was open for 10% of the time, Pallas kernels for 0%

profile of v2, /device:TPU:0, one launch (start us, length us, event | category | flops | bytes accessed | tf_op | source)
XLA Modules:
  0.0 428.2 jit_solution(10332687316284777622)
XLA Ops:
  7.2 5.8 %multiply_reduce_fusion.1 = f32[2,2048]{1,0:T(2,128)S(1)} fusion(bf16[2,1024,2048]{2,1,0:T(8,128)(2,1)} %param.5), kind=kLoop, calls=%fused_computation.1 | loop fusion | flops 12578816 | bytes 8404992 | tf_op jit(solution)/shard_map/reduce_sum | solution.py:92
  13.0 4.2 fusion.238
  18.5 5.6 %multiply_reduce_fusion = f32[2,2048]{1,0:T(2,128)S(1)} fusion(bf16[2,1024,2048]{2,1,0:T(8,128)(2,1)} %param.6), kind=kLoop, calls=%fused_computation | loop fusion | flops 12578816 | bytes 8404992 | tf_op jit(solution)/shard_map/reduce_sum | solution.py:92
  26.0 13.1 %device_total.2 = f32[2,8,128]{2,1,0:T(8,128)} custom-call(f32[8,128]{1,0:T(8,128)} %broadcast_in_dim.6.value_ref), custom_call_target="tpu_custom_call" | custom-call | tf_op jit(solution)/shard_map/device_total/pallas_call | solution.py:66
  41.0 3.7 fusion.73
  44.9 4.7 %fusion.76 = f16[256,2048]{1,0:T(8,128)(2,1)} fusion(f32[]{:T(128)} %bitcast.3, bf16[2,1024,2048]{2,1,0:T(8,128)(2,1)} %param.6, bf16[1,1024,2048]{2,1,0:T(8,128)(2,1)} %get-tuple-element.18, s32[]{:T(128)S(6)} %select_n.57), kind=kOutput, calls=%fused_computation.90 | convolution fusion | flops 1075838976 | bytes 5767684 | tf_op jit(solution)/shard_map/tr,tc->rc/dot_general | solution.py:114
  50.0 5.1 %fusion.159 = f16[256,2048]{1,0:T(8,128)(2,1)S(1)} fusion(f16[256,2048]{1,0:T(8,128)(2,1)S(1)} %collective-permute-done, f32[]{:T(128)} %bitcast.4, f32[]{:T(128)} %bitcast.3, bf16[2,1024,2048]{2,1,0:T(8,128)(2,1)} %param.6, bf16[1,1024,2048]{2,1,0:T(8,128)(2,1)} %get-tuple-element.19, s32[]{:T(128)S(6)} %select_n.54), kind=kOutput, calls=%fused_computation.159 | convolution fusion | flops 1078984704 | bytes 6816772 | tf_op jit(solution)/shard_map/tr,tc->rc/dot_general | solution.py:114
  55.1 5.1 %fusion.160 = f16[256,2048]{1,0:T(8,128)(2,1)S(1)} fusion(f16[256,2048]{1,0:T(8,128)(2,1)S(1)} %collective-permute-done.1, f32[]{:T(128)} %bitcast.4, f32[]{:T(128)} %bitcast.3, bf16[2,1024,2048]{2,1,0:T(8,128)(2,1)} %param.6, bf16[1,1024,2048]{2,1,0:T(8,128)(2,1)} %get-tuple-element.18, s32[]{:T(128)S(6)} %select_n.56), kind=kOutput, calls=%fused_computation.160 | convolution fusion | flops 1078984704 | bytes 6816772 | tf_op jit(solution)/shard_map/tr,tc->rc/dot_general | solution.py:114
  60.9 3.1 collective-permute-start.11
  65.5 1.4 fusion.85
  76.9 11.2 %collective-permute-done.5 = f16[256,2048]{1,0:T(8,128)(2,1)S(1)} collective-permute-done((f16[256,2048]{1,0:T(8,128)(2,1)S(1)}, f16[256,2048]{1,0:T(8,128)(2,1)S(1)}, u32[]{:S(2)}, u32[]{:S(2)}) %collective-permute-start.5) | collective-permute-done | bytes 1048608 | tf_op jit(solution)/shard_map/ppermute | solution.py:131
  88.6 2.9 fusion.161
  91.5 16.8 %collective-permute-done.11 = f16[256,2048]{1,0:T(8,128)(2,1)S(1)} collective-permute-done((f16[256,2048]{1,0:T(8,128)(2,1)S(1)}, f16[256,2048]{1,0:T(8,128)(2,1)S(1)}, u32[]{:S(2)}, u32[]{:S(2)}) %collective-permute-start.11) | collective-permute-done | bytes 1048608 | tf_op jit(solution)/shard_map/ppermute | solution.py:131
  108.3 1.8 collective-permute-start.6
  110.1 2.9 fusion.163
  113.0 4.2 collective-permute-start.12
  118.5 1.4 fusion.79
  119.9 18.4 %collective-permute-done.6 = f16[256,2048]{1,0:T(8,128)(2,1)S(1)} collective-permute-done((f16[256,2048]{1,0:T(8,128)(2,1)S(1)}, f16[256,2048]{1,0:T(8,128)(2,1)S(1)}, u32[]{:S(2)}, u32[]{:S(2)}) %collective-permute-start.6) | collective-permute-done | bytes 1048608 | tf_op jit(solution)/shard_map/ppermute | solution.py:135
  138.3 2.9 fusion.162
  141.3 18.6 %collective-permute-done.12 = f16[256,2048]{1,0:T(8,128)(2,1)S(1)} collective-permute-done((f16[256,2048]{1,0:T(8,128)(2,1)S(1)}, f16[256,2048]{1,0:T(8,128)(2,1)S(1)}, u32[]{:S(2)}, u32[]{:S(2)}) %collective-permute-start.12) | collective-permute-done | bytes 1048608 | tf_op jit(solution)/shard_map/ppermute | solution.py:135
  159.9 2.9 fusion.164
  162.7 5.3 %collective-permute-start.13 = (f16[256,2048]{1,0:T(8,128)(2,1)S(1)}, f16[256,2048]{1,0:T(8,128)(2,1)S(1)}, u32[]{:S(2)}, u32[]{:S(2)}) collective-permute-start(f16[256,2048]{1,0:T(8,128)(2,1)S(1)} %fusion.164), channel_id=1, source_target_pairs={{0,6},{1,7},{2,0},{3,1},{4,2},{5,3},{6,4},{7,5},{8,14},{9,15},{10,... | collective-permute-start | bytes 3145736 | tf_op jit(solution)/shard_map/ppermute | solution.py:135
  170.6 18.1 %collective-permute-done.7 = f16[256,2048]{1,0:T(8,128)(2,1)S(1)} collective-permute-done((f16[256,2048]{1,0:T(8,128)(2,1)S(1)}, f16[256,2048]{1,0:T(8,128)(2,1)S(1)}, u32[]{:S(2)}, u32[]{:S(2)}) %collective-permute-start.7) | collective-permute-done | bytes 1048608 | tf_op jit(solution)/shard_map/ppermute | solution.py:135
  188.8 3.3 multiply_reduce_fusion.3
  192.1 2.2 copy.13
  194.2 15.4 %collective-permute-done.13 = f16[256,2048]{1,0:T(8,128)(2,1)S(1)} collective-permute-done((f16[256,2048]{1,0:T(8,128)(2,1)S(1)}, f16[256,2048]{1,0:T(8,128)(2,1)S(1)}, u32[]{:S(2)}, u32[]{:S(2)}) %collective-permute-start.13) | collective-permute-done | bytes 1048608 | tf_op jit(solution)/shard_map/ppermute | solution.py:135
  209.6 3.3 multiply_reduce_fusion.2
  212.9 2.8 stack.10
  217.6 15.4 %device_total.3 = f32[2,8,128]{2,1,0:T(8,128)} custom-call(f32[8,128]{1,0:T(8,128)} %broadcast_in_dim.7.value_ref), custom_call_target="tpu_custom_call" | custom-call | tf_op jit(solution)/shard_map/device_total/pallas_call | solution.py:66
  234.9 20.8 %fusion.234 = (bf16[256,2,2048]{2,1,0:T(2,128)(2,1)}, f32[256,2,2048]{2,1,0:T(2,128)}, f32[256,2,2048]{2,1,0:T(2,128)}, f32[256,2,2048]{2,1,0:T(2,128)}) fusion(f32[256,2,2048]{2,1,0:T(2,128)} %param.7, f32[256,1,2048]{2,1,0:T(1,128)} %stack.10, f32[256,1,2048]{2,1,0:T(1,128)S(1)} %copy.13, f32[]{:T(128)} %bitcast.20, f32[256,2,2048]{2,1,0:T(2,128)} %param.8, ...), kind=kLoop, calls=%fused_computation.232 | loop fusion | flops 18874368 | bytes 31457284 | tf_op jit(solution)/shard_map/convert_element_type | solution.py:161
  255.7 151.4 %all-gather.2.cloned.1.call-done = bf16[2048,2,2048]{2,1,0:T(2,128)(2,1)} async-done(((bf16[256,2,2048]{2,1,0:T(2,128)(2,1)}), bf16[2048,2,2048]{2,1,0:T(2,128)(2,1)}) %all-gather.2.cloned.1.call-update) | async-done | bytes 16777232 | tf_op jit(solution)/shard_map/all_gather | solution.py:162
  407.1 14.1 %copy.15 = bf16[2048,2,2048]{2,1,0:T(2,128)(2,1)} copy(bf16[2048,2,2048]{2,1,0:T(2,128)(2,1)} %all-gather.2.cloned.1.call-done) | data formatting | bytes 33554432
  (49 shorter events, 22.1 us)
Async XLA Ops:
  7.2 399.9 %all-gather.2.cloned.1.call-start = ((), (), s32[]{:S(2)}) async-start(), calls=%async_computation | async-start | bytes 18874368 | tf_op jit(solution)/shard_map/all_gather | solution.py:162
  7.2 5.8 %copy-start = (bf16[2,1024,2048]{2,1,0:T(8,128)(2,1)S(1)}, bf16[2,1024,2048]{2,1,0:T(8,128)(2,1)}, u32[]{:S(2)}) copy-start(bf16[2,1024,2048]{2,1,0:T(8,128)(2,1)} %param.5) | copy-start | bytes 25165828
  44.7 5.3 %collective-permute-start = (f16[256,2048]{1,0:T(8,128)(2,1)S(1)}, f16[256,2048]{1,0:T(8,128)(2,1)S(1)}, u32[]{:S(2)}, u32[]{:S(2)}) collective-permute-start(f16[256,2048]{1,0:T(8,128)(2,1)S(1)} %fusion.73), channel_id=1, source_target_pairs={{0,1},{1,0},{2,3},{3,2},{4,5},{5,4},{6,7},{7,6},{8,9},{9,8},{10,11... | collective-permute-start | bytes 3145736 | tf_op jit(solution)/shard_map/ppermute | solution.py:120
  49.6 5.5 %collective-permute-start.1 = (f16[256,2048]{1,0:T(8,128)(2,1)}, f16[256,2048]{1,0:T(8,128)(2,1)S(1)}, u32[]{:S(2)}, u32[]{:S(2)}) collective-permute-start(f16[256,2048]{1,0:T(8,128)(2,1)} %fusion.76), channel_id=1, source_target_pairs={{0,1},{1,0},{2,3},{3,2},{4,5},{5,4},{6,7},{7,6},{8,9},{9,8},{10,11... | collective-permute-start | bytes 3145736 | tf_op jit(solution)/shard_map/ppermute | solution.py:120
  50.0 14.1 %slice-start = ((s8[8388608]{0:T(1024)(128)(4,1)}), s8[4194304]{0:T(1024)(128)(4,1)S(1)}, s32[]{:S(2)}) async-start(s8[8388608]{0:T(1024)(128)(4,1)} %bitcast.139), calls=%async_computation.1 | async-start | bytes 8388608
  55.0 9.0 %slice-start.1 = ((s8[8388608]{0:T(1024)(128)(4,1)}), s8[4194304]{0:T(1024)(128)(4,1)S(1)}, s32[]{:S(2)}) async-start(s8[8388608]{0:T(1024)(128)(4,1)} %bitcast.139), calls=%async_computation.2 | async-start | bytes 8388608
  55.1 10.4 %slice-start.2 = ((s8[8388608]{0:T(1024)(128)(4,1)}), s8[4194304]{0:T(1024)(128)(4,1)S(1)}, s32[]{:S(2)}) async-start(s8[8388608]{0:T(1024)(128)(4,1)} %bitcast.141), calls=%async_computation.3 | async-start | bytes 8388608
  60.2 5.3 %slice-start.3 = ((s8[8388608]{0:T(1024)(128)(4,1)}), s8[4194304]{0:T(1024)(128)(4,1)S(1)}, s32[]{:S(2)}) async-start(s8[8388608]{0:T(1024)(128)(4,1)} %bitcast.141), calls=%async_computation.4 | async-start | bytes 8388608
  60.2 27.9 %collective-permute-start.5 = (f16[256,2048]{1,0:T(8,128)(2,1)S(1)}, f16[256,2048]{1,0:T(8,128)(2,1)S(1)}, u32[]{:S(2)}, u32[]{:S(2)}) collective-permute-start(f16[256,2048]{1,0:T(8,128)(2,1)S(1)} %fusion.159), channel_id=1, source_target_pairs={{0,2},{1,3},{2,4},{3,5},{4,6},{5,7},{6,0},{7,1},{8,10},{9,11},{10,... | collective-permute-start | bytes 3145736 | tf_op jit(solution)/shard_map/ppermute | solution.py:131
  60.9 47.4 %collective-permute-start.11 = (f16[256,2048]{1,0:T(8,128)(2,1)S(1)}, f16[256,2048]{1,0:T(8,128)(2,1)S(1)}, u32[]{:S(2)}, u32[]{:S(2)}) collective-permute-start(f16[256,2048]{1,0:T(8,128)(2,1)S(1)} %fusion.160), channel_id=1, source_target_pairs={{0,6},{1,7},{2,0},{3,1},{4,2},{5,3},{6,4},{7,5},{8,14},{9,15},{10,... | collective-permute-start | bytes 3145736 | tf_op jit(solution)/shard_map/ppermute | solution.py:131
  71.0 123.3 %collective-permute-start.8 = (f16[256,2048]{1,0:T(8,128)(2,1)S(1)}, f16[256,2048]{1,0:T(8,128)(2,1)S(1)}, u32[]{:S(2)}, u32[]{:S(2)}) collective-permute-start(f16[256,2048]{1,0:T(8,128)(2,1)S(1)} %fusion.88), channel_id=1, source_target_pairs={{0,1},{1,0},{2,3},{3,2},{4,5},{5,4},{6,7},{7,6},{8,9},{9,8},{10,11... | collective-permute-start | bytes 3145736 | tf_op jit(solution)/shard_map/ppermute | solution.py:120
  71.1 39.0 %collective-permute-start.10 = (f16[256,2048]{1,0:T(8,128)(2,1)S(1)}, f16[256,2048]{1,0:T(8,128)(2,1)S(1)}, u32[]{:S(2)}, u32[]{:S(2)}) collective-permute-start(f16[256,2048]{1,0:T(8,128)(2,1)S(1)} %fusion.94), channel_id=1, source_target_pairs={{0,1},{1,0},{2,3},{3,2},{4,5},{5,4},{6,7},{7,6},{8,9},{9,8},{10,11... | collective-permute-start | bytes 3145736 | tf_op jit(solution)/shard_map/ppermute | solution.py:120
  71.6 16.6 %collective-permute-start.4 = (f16[256,2048]{1,0:T(8,128)(2,1)S(1)}, f16[256,2048]{1,0:T(8,128)(2,1)S(1)}, u32[]{:S(2)}, u32[]{:S(2)}) collective-permute-start(f16[256,2048]{1,0:T(8,128)(2,1)S(1)} %fusion.85), channel_id=1, source_target_pairs={{0,1},{1,0},{2,3},{3,2},{4,5},{5,4},{6,7},{7,6},{8,9},{9,8},{10,11... | collective-permute-start | bytes 3145736 | tf_op jit(solution)/shard_map/ppermute | solution.py:120
  88.1 53.1 %collective-permute-start.9 = (f16[256,2048]{1,0:T(8,128)(2,1)S(1)}, f16[256,2048]{1,0:T(8,128)(2,1)S(1)}, u32[]{:S(2)}, u32[]{:S(2)}) collective-permute-start(f16[256,2048]{1,0:T(8,128)(2,1)S(1)} %fusion.91), channel_id=1, source_target_pairs={{0,1},{1,0},{2,3},{3,2},{4,5},{5,4},{6,7},{7,6},{8,9},{9,8},{10,11... | collective-permute-start | bytes 3145736 | tf_op jit(solution)/shard_map/ppermute | solution.py:120
  88.1 31.7 %collective-permute-start.3 = (f16[256,2048]{1,0:T(8,128)(2,1)S(1)}, f16[256,2048]{1,0:T(8,128)(2,1)S(1)}, u32[]{:S(2)}, u32[]{:S(2)}) collective-permute-start(f16[256,2048]{1,0:T(8,128)(2,1)S(1)} %fusion.82), channel_id=1, source_target_pairs={{0,1},{1,0},{2,3},{3,2},{4,5},{5,4},{6,7},{7,6},{8,9},{9,8},{10,11... | collective-permute-start | bytes 3145736 | tf_op jit(solution)/shard_map/ppermute | solution.py:120
  108.3 30.0 %collective-permute-start.6 = (f16[256,2048]{1,0:T(8,128)(2,1)S(1)}, f16[256,2048]{1,0:T(8,128)(2,1)S(1)}, u32[]{:S(2)}, u32[]{:S(2)}) collective-permute-start(f16[256,2048]{1,0:T(8,128)(2,1)S(1)} %fusion.161), channel_id=1, source_target_pairs={{0,2},{1,3},{2,4},{3,5},{4,6},{5,7},{6,0},{7,1},{8,10},{9,11},{10,... | collective-permute-start | bytes 3145736 | tf_op jit(solution)/shard_map/ppermute | solution.py:135
  113.0 46.9 %collective-permute-start.12 = (f16[256,2048]{1,0:T(8,128)(2,1)S(1)}, f16[256,2048]{1,0:T(8,128)(2,1)S(1)}, u32[]{:S(2)}, u32[]{:S(2)}) collective-permute-start(f16[256,2048]{1,0:T(8,128)(2,1)S(1)} %fusion.163), channel_id=1, source_target_pairs={{0,6},{1,7},{2,0},{3,1},{4,2},{5,3},{6,4},{7,5},{8,14},{9,15},{10,... | collective-permute-start | bytes 3145736 | tf_op jit(solution)/shard_map/ppermute | solution.py:135
  119.8 50.8 %collective-permute-start.2 = (f16[256,2048]{1,0:T(8,128)(2,1)S(1)}, f16[256,2048]{1,0:T(8,128)(2,1)S(1)}, u32[]{:S(2)}, u32[]{:S(2)}) collective-permute-start(f16[256,2048]{1,0:T(8,128)(2,1)S(1)} %fusion.79), channel_id=1, source_target_pairs={{0,1},{1,0},{2,3},{3,2},{4,5},{5,4},{6,7},{7,6},{8,9},{9,8},{10,11... | collective-permute-start | bytes 3145736 | tf_op jit(solution)/shard_map/ppermute | solution.py:120
  141.2 47.6 %collective-permute-start.7 = (f16[256,2048]{1,0:T(8,128)(2,1)S(1)}, f16[256,2048]{1,0:T(8,128)(2,1)S(1)}, u32[]{:S(2)}, u32[]{:S(2)}) collective-permute-start(f16[256,2048]{1,0:T(8,128)(2,1)S(1)} %fusion.162), channel_id=1, source_target_pairs={{0,2},{1,3},{2,4},{3,5},{4,6},{5,7},{6,0},{7,1},{8,10},{9,11},{10,... | collective-permute-start | bytes 3145736 | tf_op jit(solution)/shard_map/ppermute | solution.py:135
  162.7 46.9 %collective-permute-start.13 = (f16[256,2048]{1,0:T(8,128)(2,1)S(1)}, f16[256,2048]{1,0:T(8,128)(2,1)S(1)}, u32[]{:S(2)}, u32[]{:S(2)}) collective-permute-start(f16[256,2048]{1,0:T(8,128)(2,1)S(1)} %fusion.164), channel_id=1, source_target_pairs={{0,6},{1,7},{2,0},{3,1},{4,2},{5,3},{6,4},{7,5},{8,14},{9,15},{10,... | collective-permute-start | bytes 3145736 | tf_op jit(solution)/shard_map/ppermute | solution.py:135
Sparse Core Ops, SparseCore 0:
  255.8 151.1 all-gather.1

commit v3 on v2

--- a/solution.py
+++ b/solution.py
@@ -155,12 +155,19 @@
     limit = limit_scale * math.sqrt(entries)
     clip_factor = limit / jnp.maximum(jnp.sqrt(sum_squares), limit)
     grad_own = with_layout_constraint(jnp.stack(layer_grads, axis=1), Layout((0, 1, 2)))
-    new_master, new_first, new_second = adam_update(
-        grad_own, master, first_moment, second_moment, clip_factor
-    )
-    rounded = new_master.astype(jnp.bfloat16)
-    tp_rows = lax.all_gather(rounded, "dp", axis=0, tiled=True)
-    return (new_master, new_first, new_second, tp_rows)
+    states = (grad_own, master, first_moment, second_moment)
+    cut = own_rows // 2
+    head = adam_update(*(x[:cut] for x in states), clip_factor)[0].astype(jnp.bfloat16)
+    clip_factor, head = lax.optimization_barrier((clip_factor, head))
+    head_rows = lax.all_gather(head, "dp", axis=0)
+    new_master, new_first, new_second = adam_update(*states, clip_factor)
+    tail = new_master[cut:].astype(jnp.bfloat16)
+    tail_rows = lax.all_gather(tail, "dp", axis=0)
+    tp_rows = jnp.zeros((lax.axis_size("dp"),) + master.shape, jnp.bfloat16)
+    tp_rows = lax.dynamic_update_slice_in_dim(tp_rows, head_rows, 0, 1)
+    tp_rows = lax.optimization_barrier(tp_rows)
+    tp_rows = lax.dynamic_update_slice_in_dim(tp_rows, tail_rows, cut, 1)
+    return (new_master, new_first, new_second, tp_rows.reshape((-1,) + master.shape[1:]))
 
 
 def solution(mesh):

time: 431 us -> 428 us (level)
  waiting for transfers between devices: 250 us -> 226 us
  local copies, waits for them, and re-layouts: 28.2 us -> 39.2 us
  other arithmetic: 51.5 us -> 61 us
    all_gather x1 -> x2, waiting for transfers between devices: 151 us -> 128 us  [the longest x1 69 us: on_device(): tail_rows = lax.all_gather(tail, 'dp', axis=0)]
    dynamic_update_slice x0 -> x2, local copies, waits for them, and re-layouts: none -> 21.2 us  [the longest x1 13.2 us: on_device(): tp_rows = lax.dynamic_update_slice_in_dim(tp_rows, head_rows, 0, 1)]
    sub x0 -> x1, other arithmetic: none -> 19.7 us  [adam_update(): new_master = master - learn_rate * (step_dir + decay_rate * master)]
    unnamed x11 -> x12, local copies, waits for them, and re-layouts: 14.2 us -> 2.05 us
    convert_element_type x1, other arithmetic: 20.8 us -> 10.6 us  [on_device(): adam_update(*(x[:cut] for x in states), clip_factor)[0].astype(jnp.bfloat16)]
  transfers between devices with their start and end apart: 15 -> 16, of which waited for: 7 -> 8; matrix products, arithmetic and copies ran while one was open for 10% -> 19% of each run, Pallas kernels for 0% -> 0%
where the time goes in v3:
time: 428 us; the launch traced here: 425 us
  waiting for transfers between devices  226 us (53%)
  other arithmetic  61 us (14%)
  local copies, waits for them, and re-layouts  39.2 us (9%)
  matrix products  34.5 us (8%)
  Pallas kernels  28.5 us (7%)
  between operations  18.6 us (4%)
  starting transfers between devices  17.1 us (4%)
    ppermute x4, waiting for transfers between devices, reduce_rows(): lax.ppermute(pack(values[i]), 'dp', rings[i])  70.5 us
    all_gather x1, waiting for transfers between devices, on_device(): tail_rows = lax.all_gather(tail, 'dp', axis=0)  69 us
    all_gather x1, waiting for transfers between devices, on_device(): head_rows = lax.all_gather(head, 'dp', axis=0)  58.6 us
    dot_general x16, matrix products, product(): jnp.einsum('tr,tc->rc', acts, out_grads[layer], preferred_element_type=jn...  34.5 us
    pallas_call x2, Pallas kernels, device_total(): pl.pallas_call(functools.partial(total_kernel, n_tp, n_dp), out_shape=jax...  28.5 us
    ppermute x2, waiting for transfers between devices, reduce_rows(): running = [lax.ppermute(first[i], 'dp', rings[i]) for i in range(layers)]  28 us
    sub x1, other arithmetic, adam_update(): new_master = master - learn_rate * (step_dir + decay_rate * master)  19.7 us
    dynamic_update_slice x1, local copies, waits for them, and re-layouts, on_device(): tp_rows = lax.dynamic_update_slice_in_dim(tp_rows, head_rows, 0, 1)  13.2 us
  transfers between devices with their start and end apart: 16, of which 8 were waited for; matrix products, arithmetic and copies ran while one was open for 19% of the time, Pallas kernels for 0%

profile of v3, /device:TPU:0, one launch (start us, length us, event | category | flops | bytes accessed | tf_op | source)
XLA Modules:
  0.0 425.0 jit_solution(9370648488881770730)
XLA Ops:
  7.2 5.8 %multiply_reduce_fusion.1 = f32[2,2048]{1,0:T(2,128)S(1)} fusion(bf16[2,1024,2048]{2,1,0:T(8,128)(2,1)} %param.5), kind=kLoop, calls=%fused_computation.1 | loop fusion | flops 12578816 | bytes 8404992 | tf_op jit(solution)/shard_map/reduce_sum | solution.py:92
  13.0 4.2 fusion.243
  18.5 5.6 %multiply_reduce_fusion = f32[2,2048]{1,0:T(2,128)S(1)} fusion(bf16[2,1024,2048]{2,1,0:T(8,128)(2,1)} %param.6), kind=kLoop, calls=%fused_computation | loop fusion | flops 12578816 | bytes 8404992 | tf_op jit(solution)/shard_map/reduce_sum | solution.py:92
  26.0 13.1 %device_total.2 = f32[2,8,128]{2,1,0:T(8,128)} custom-call(f32[8,128]{1,0:T(8,128)} %broadcast_in_dim.7.value_ref), custom_call_target="tpu_custom_call" | custom-call | tf_op jit(solution)/shard_map/device_total/pallas_call | solution.py:66
  41.0 3.7 fusion.74
  44.9 4.7 %fusion.77 = f16[256,2048]{1,0:T(8,128)(2,1)} fusion(f32[]{:T(128)} %bitcast.3, bf16[2,1024,2048]{2,1,0:T(8,128)(2,1)} %param.6, bf16[1,1024,2048]{2,1,0:T(8,128)(2,1)} %get-tuple-element.21, s32[]{:T(128)S(6)} %select_n.57), kind=kOutput, calls=%fused_computation.94 | convolution fusion | flops 1075838976 | bytes 5767684 | tf_op jit(solution)/shard_map/tr,tc->rc/dot_general | solution.py:114
  50.0 5.1 %fusion.160 = f16[256,2048]{1,0:T(8,128)(2,1)S(1)} fusion(f16[256,2048]{1,0:T(8,128)(2,1)S(1)} %collective-permute-done, f32[]{:T(128)} %bitcast.4, f32[]{:T(128)} %bitcast.3, bf16[2,1024,2048]{2,1,0:T(8,128)(2,1)} %param.6, bf16[1,1024,2048]{2,1,0:T(8,128)(2,1)} %get-tuple-element.22, s32[]{:T(128)S(6)} %select_n.54), kind=kOutput, calls=%fused_computation.163 | convolution fusion | flops 1078984704 | bytes 6816772 | tf_op jit(solution)/shard_map/tr,tc->rc/dot_general | solution.py:114
  55.1 5.1 %fusion.161 = f16[256,2048]{1,0:T(8,128)(2,1)S(1)} fusion(f16[256,2048]{1,0:T(8,128)(2,1)S(1)} %collective-permute-done.1, f32[]{:T(128)} %bitcast.4, f32[]{:T(128)} %bitcast.3, bf16[2,1024,2048]{2,1,0:T(8,128)(2,1)} %param.6, bf16[1,1024,2048]{2,1,0:T(8,128)(2,1)} %get-tuple-element.21, s32[]{:T(128)S(6)} %select_n.56), kind=kOutput, calls=%fused_computation.164 | convolution fusion | flops 1078984704 | bytes 6816772 | tf_op jit(solution)/shard_map/tr,tc->rc/dot_general | solution.py:114
  60.9 3.1 collective-permute-start.11
  76.9 11.2 %collective-permute-done.5 = f16[256,2048]{1,0:T(8,128)(2,1)S(1)} collective-permute-done((f16[256,2048]{1,0:T(8,128)(2,1)S(1)}, f16[256,2048]{1,0:T(8,128)(2,1)S(1)}, u32[]{:S(2)}, u32[]{:S(2)}) %collective-permute-start.5) | collective-permute-done | bytes 1048608 | tf_op jit(solution)/shard_map/ppermute | solution.py:131
  88.6 2.9 fusion.167
  91.5 16.8 %collective-permute-done.11 = f16[256,2048]{1,0:T(8,128)(2,1)S(1)} collective-permute-done((f16[256,2048]{1,0:T(8,128)(2,1)S(1)}, f16[256,2048]{1,0:T(8,128)(2,1)S(1)}, u32[]{:S(2)}, u32[]{:S(2)}) %collective-permute-start.11) | collective-permute-done | bytes 1048608 | tf_op jit(solution)/shard_map/ppermute | solution.py:131
  110.1 2.9 fusion.169
  113.0 4.2 collective-permute-start.12
  119.9 18.4 %collective-permute-done.6 = f16[256,2048]{1,0:T(8,128)(2,1)S(1)} collective-permute-done((f16[256,2048]{1,0:T(8,128)(2,1)S(1)}, f16[256,2048]{1,0:T(8,128)(2,1)S(1)}, u32[]{:S(2)}, u32[]{:S(2)}) %collective-permute-start.6) | collective-permute-done | bytes 1048608 | tf_op jit(solution)/shard_map/ppermute | solution.py:135
  138.3 2.9 fusion.168
  141.3 18.6 %collective-permute-done.12 = f16[256,2048]{1,0:T(8,128)(2,1)S(1)} collective-permute-done((f16[256,2048]{1,0:T(8,128)(2,1)S(1)}, f16[256,2048]{1,0:T(8,128)(2,1)S(1)}, u32[]{:S(2)}, u32[]{:S(2)}) %collective-permute-start.12) | collective-permute-done | bytes 1048608 | tf_op jit(solution)/shard_map/ppermute | solution.py:135
  159.9 2.9 fusion.170
  162.7 5.3 %collective-permute-start.13 = (f16[256,2048]{1,0:T(8,128)(2,1)S(1)}, f16[256,2048]{1,0:T(8,128)(2,1)S(1)}, u32[]{:S(2)}, u32[]{:S(2)}) collective-permute-start(f16[256,2048]{1,0:T(8,128)(2,1)S(1)} %fusion.170), channel_id=1, source_target_pairs={{0,6},{1,7},{2,0},{3,1},{4,2},{5,3},{6,4},{7,5},{8,14},{9,15},{10,... | collective-permute-start | bytes 3145736 | tf_op jit(solution)/shard_map/ppermute | solution.py:135
  170.6 18.1 %collective-permute-done.7 = f16[256,2048]{1,0:T(8,128)(2,1)S(1)} collective-permute-done((f16[256,2048]{1,0:T(8,128)(2,1)S(1)}, f16[256,2048]{1,0:T(8,128)(2,1)S(1)}, u32[]{:S(2)}, u32[]{:S(2)}) %collective-permute-start.7) | collective-permute-done | bytes 1048608 | tf_op jit(solution)/shard_map/ppermute | solution.py:135
  188.8 3.3 multiply_reduce_fusion.3
  192.1 2.2 copy.14
  194.2 15.4 %collective-permute-done.13 = f16[256,2048]{1,0:T(8,128)(2,1)S(1)} collective-permute-done((f16[256,2048]{1,0:T(8,128)(2,1)S(1)}, f16[256,2048]{1,0:T(8,128)(2,1)S(1)}, u32[]{:S(2)}, u32[]{:S(2)}) %collective-permute-start.13) | collective-permute-done | bytes 1048608 | tf_op jit(solution)/shard_map/ppermute | solution.py:135
  209.6 3.3 multiply_reduce_fusion.2
  212.9 2.8 stack.10
  217.6 15.4 %device_total.3 = f32[2,8,128]{2,1,0:T(8,128)} custom-call(f32[8,128]{1,0:T(8,128)} %broadcast_in_dim.8.value_ref), custom_call_target="tpu_custom_call" | custom-call | tf_op jit(solution)/shard_map/device_total/pallas_call | solution.py:66
  234.9 10.6 %subtract_convert_fusion = bf16[128,2,2048]{2,1,0:T(2,128)(2,1)} fusion(f32[256,2,2048]{2,1,0:T(2,128)} %param.9, f32[256,1,2048]{2,1,0:T(1,128)} %stack.10, f32[256,1,2048]{2,1,0:T(1,128)S(1)} %copy.14, f32[256,2,2048]{2,1,0:T(2,128)} %param.8, f32[256,2,2048]{2,1,0:T(2,128)} %param.7, f32[]{:T(128)} %bitcast.20), kind=kLoop, calls=%fused_computation.171 | loop fusion | flops 9437184 | bytes 11534340 | tf_op jit(solution)/shard_map/convert_element_type | solution.py:160
  245.6 19.7 %multiply_subtract_fusion = (f32[256,2,2048]{2,1,0:T(2,128)S(1)}, f32[256,2,2048]{2,1,0:T(2,128)}, f32[256,2,2048]{2,1,0:T(2,128)}) fusion(f32[256,2,2048]{2,1,0:T(2,128)} %param.7, f32[256,1,2048]{2,1,0:T(1,128)} %stack.10, f32[256,1,2048]{2,1,0:T(1,128)S(1)} %copy.14, f32[]{:T(128)} %bitcast.20, f32[256,2,2048]{2,1,0:T(2,128)} %param.8, ...), kind=kLoop, calls=%fused_computation.40 | loop fusion | flops 17825792 | bytes 29360132 | tf_op jit(solution)/shard_map/sub | solution.py:144
  269.2 58.6 %all-gather.5.cloned.1.call-done = bf16[1024,2,2048]{2,1,0:T(2,128)(2,1)} async-done(((bf16[128,2,2048]{2,1,0:T(2,128)(2,1)}), bf16[1024,2,2048]{2,1,0:T(2,128)(2,1)}) %all-gather.5.cloned.1.call-update) | async-done | bytes 8388624 | tf_op jit(solution)/shard_map/all_gather | solution.py:162
  327.8 13.2 %dynamic_update_slice.6 = bf16[8,256,2,2048]{3,2,1,0:T(2,128)(2,1)} pad(bf16[8,128,2,2048]{3,2,1,0:T(2,128)(2,1)} %bitcast.147, bf16[]{:T(256)} %constant.139.clone.1), padding=0_0x0_128x0_0x0_0 | pad | bytes 25165826 | tf_op jit(solution)/shard_map/dynamic_update_slice | solution.py:167
  341.0 69.0 %all-gather.7.cloned.1.call-done = bf16[1024,2,2048]{2,1,0:T(2,128)(2,1)} async-done(((bf16[128,2,2048]{2,1,0:T(2,128)(2,1)}), bf16[1024,2,2048]{2,1,0:T(2,128)(2,1)}) %all-gather.7.cloned.1.call-update) | async-done | bytes 8388624 | tf_op jit(solution)/shard_map/all_gather | solution.py:165
  410.0 8.0 %constant_dynamic-update-slice_fusion = bf16[8,256,2,2048]{3,2,1,0:T(2,128)(2,1)} fusion(bf16[8,256,2,2048]{3,2,1,0:T(2,128)(2,1)} %dynamic_update_slice.6, bf16[8,128,2,2048]{3,2,1,0:T(2,128)(2,1)} %bitcast.148), kind=kLoop, calls=%fused_computation.226 | loop fusion | bytes 16777216 | tf_op jit(solution)/shard_map/dynamic_update_slice | solution.py:169
  (57 shorter events, 30.6 us)
Async XLA Ops:
  7.2 320.7 %all-gather.5.cloned.1.call-start = ((), (), s32[]{:S(2)}) async-start(), calls=%async_computation | async-start | bytes 9437184 | tf_op jit(solution)/shard_map/all_gather | solution.py:162
  7.2 5.8 %copy-start = (bf16[2,1024,2048]{2,1,0:T(8,128)(2,1)S(1)}, bf16[2,1024,2048]{2,1,0:T(8,128)(2,1)}, u32[]{:S(2)}) copy-start(bf16[2,1024,2048]{2,1,0:T(8,128)(2,1)} %param.5) | copy-start | bytes 25165828
  44.7 5.3 %collective-permute-start = (f16[256,2048]{1,0:T(8,128)(2,1)S(1)}, f16[256,2048]{1,0:T(8,128)(2,1)S(1)}, u32[]{:S(2)}, u32[]{:S(2)}) collective-permute-start(f16[256,2048]{1,0:T(8,128)(2,1)S(1)} %fusion.74), channel_id=1, source_target_pairs={{0,1},{1,0},{2,3},{3,2},{4,5},{5,4},{6,7},{7,6},{8,9},{9,8},{10,11... | collective-permute-start | bytes 3145736 | tf_op jit(solution)/shard_map/ppermute | solution.py:120
  49.6 5.5 %collective-permute-start.1 = (f16[256,2048]{1,0:T(8,128)(2,1)}, f16[256,2048]{1,0:T(8,128)(2,1)S(1)}, u32[]{:S(2)}, u32[]{:S(2)}) collective-permute-start(f16[256,2048]{1,0:T(8,128)(2,1)} %fusion.77), channel_id=1, source_target_pairs={{0,1},{1,0},{2,3},{3,2},{4,5},{5,4},{6,7},{7,6},{8,9},{9,8},{10,11... | collective-permute-start | bytes 3145736 | tf_op jit(solution)/shard_map/ppermute | solution.py:120
  50.0 14.1 %slice-start = ((s8[8388608]{0:T(1024)(128)(4,1)}), s8[4194304]{0:T(1024)(128)(4,1)S(1)}, s32[]{:S(2)}) async-start(s8[8388608]{0:T(1024)(128)(4,1)} %bitcast.142), calls=%async_computation.2 | async-start | bytes 8388608
  55.0 9.0 %slice-start.1 = ((s8[8388608]{0:T(1024)(128)(4,1)}), s8[4194304]{0:T(1024)(128)(4,1)S(1)}, s32[]{:S(2)}) async-start(s8[8388608]{0:T(1024)(128)(4,1)} %bitcast.142), calls=%async_computation.3 | async-start | bytes 8388608
  55.1 10.4 %slice-start.2 = ((s8[8388608]{0:T(1024)(128)(4,1)}), s8[4194304]{0:T(1024)(128)(4,1)S(1)}, s32[]{:S(2)}) async-start(s8[8388608]{0:T(1024)(128)(4,1)} %bitcast.145), calls=%async_computation.4 | async-start | bytes 8388608
  60.2 5.3 %slice-start.3 = ((s8[8388608]{0:T(1024)(128)(4,1)}), s8[4194304]{0:T(1024)(128)(4,1)S(1)}, s32[]{:S(2)}) async-start(s8[8388608]{0:T(1024)(128)(4,1)} %bitcast.145), calls=%async_computation.5 | async-start | bytes 8388608
  60.2 27.9 %collective-permute-start.5 = (f16[256,2048]{1,0:T(8,128)(2,1)S(1)}, f16[256,2048]{1,0:T(8,128)(2,1)S(1)}, u32[]{:S(2)}, u32[]{:S(2)}) collective-permute-start(f16[256,2048]{1,0:T(8,128)(2,1)S(1)} %fusion.160), channel_id=1, source_target_pairs={{0,2},{1,3},{2,4},{3,5},{4,6},{5,7},{6,0},{7,1},{8,10},{9,11},{10,... | collective-permute-start | bytes 3145736 | tf_op jit(solution)/shard_map/ppermute | solution.py:131
  60.9 47.4 %collective-permute-start.11 = (f16[256,2048]{1,0:T(8,128)(2,1)S(1)}, f16[256,2048]{1,0:T(8,128)(2,1)S(1)}, u32[]{:S(2)}, u32[]{:S(2)}) collective-permute-start(f16[256,2048]{1,0:T(8,128)(2,1)S(1)} %fusion.161), channel_id=1, source_target_pairs={{0,6},{1,7},{2,0},{3,1},{4,2},{5,3},{6,4},{7,5},{8,14},{9,15},{10,... | collective-permute-start | bytes 3145736 | tf_op jit(solution)/shard_map/ppermute | solution.py:131
  71.0 123.2 %collective-permute-start.8 = (f16[256,2048]{1,0:T(8,128)(2,1)S(1)}, f16[256,2048]{1,0:T(8,128)(2,1)S(1)}, u32[]{:S(2)}, u32[]{:S(2)}) collective-permute-start(f16[256,2048]{1,0:T(8,128)(2,1)S(1)} %fusion.89), channel_id=1, source_target_pairs={{0,1},{1,0},{2,3},{3,2},{4,5},{5,4},{6,7},{7,6},{8,9},{9,8},{10,11... | collective-permute-start | bytes 3145736 | tf_op jit(solution)/shard_map/ppermute | solution.py:120
  71.1 39.0 %collective-permute-start.10 = (f16[256,2048]{1,0:T(8,128)(2,1)S(1)}, f16[256,2048]{1,0:T(8,128)(2,1)S(1)}, u32[]{:S(2)}, u32[]{:S(2)}) collective-permute-start(f16[256,2048]{1,0:T(8,128)(2,1)S(1)} %fusion.95), channel_id=1, source_target_pairs={{0,1},{1,0},{2,3},{3,2},{4,5},{5,4},{6,7},{7,6},{8,9},{9,8},{10,11... | collective-permute-start | bytes 3145736 | tf_op jit(solution)/shard_map/ppermute | solution.py:120
  71.6 16.6 %collective-permute-start.4 = (f16[256,2048]{1,0:T(8,128)(2,1)S(1)}, f16[256,2048]{1,0:T(8,128)(2,1)S(1)}, u32[]{:S(2)}, u32[]{:S(2)}) collective-permute-start(f16[256,2048]{1,0:T(8,128)(2,1)S(1)} %fusion.86), channel_id=1, source_target_pairs={{0,1},{1,0},{2,3},{3,2},{4,5},{5,4},{6,7},{7,6},{8,9},{9,8},{10,11... | collective-permute-start | bytes 3145736 | tf_op jit(solution)/shard_map/ppermute | solution.py:120
  88.1 53.1 %collective-permute-start.9 = (f16[256,2048]{1,0:T(8,128)(2,1)S(1)}, f16[256,2048]{1,0:T(8,128)(2,1)S(1)}, u32[]{:S(2)}, u32[]{:S(2)}) collective-permute-start(f16[256,2048]{1,0:T(8,128)(2,1)S(1)} %fusion.92), channel_id=1, source_target_pairs={{0,1},{1,0},{2,3},{3,2},{4,5},{5,4},{6,7},{7,6},{8,9},{9,8},{10,11... | collective-permute-start | bytes 3145736 | tf_op jit(solution)/shard_map/ppermute | solution.py:120
  88.1 31.7 %collective-permute-start.3 = (f16[256,2048]{1,0:T(8,128)(2,1)S(1)}, f16[256,2048]{1,0:T(8,128)(2,1)S(1)}, u32[]{:S(2)}, u32[]{:S(2)}) collective-permute-start(f16[256,2048]{1,0:T(8,128)(2,1)S(1)} %fusion.83), channel_id=1, source_target_pairs={{0,1},{1,0},{2,3},{3,2},{4,5},{5,4},{6,7},{7,6},{8,9},{9,8},{10,11... | collective-permute-start | bytes 3145736 | tf_op jit(solution)/shard_map/ppermute | solution.py:120
  108.3 30.0 %collective-permute-start.6 = (f16[256,2048]{1,0:T(8,128)(2,1)S(1)}, f16[256,2048]{1,0:T(8,128)(2,1)S(1)}, u32[]{:S(2)}, u32[]{:S(2)}) collective-permute-start(f16[256,2048]{1,0:T(8,128)(2,1)S(1)} %fusion.167), channel_id=1, source_target_pairs={{0,2},{1,3},{2,4},{3,5},{4,6},{5,7},{6,0},{7,1},{8,10},{9,11},{10,... | collective-permute-start | bytes 3145736 | tf_op jit(solution)/shard_map/ppermute | solution.py:135
  113.0 46.9 %collective-permute-start.12 = (f16[256,2048]{1,0:T(8,128)(2,1)S(1)}, f16[256,2048]{1,0:T(8,128)(2,1)S(1)}, u32[]{:S(2)}, u32[]{:S(2)}) collective-permute-start(f16[256,2048]{1,0:T(8,128)(2,1)S(1)} %fusion.169), channel_id=1, source_target_pairs={{0,6},{1,7},{2,0},{3,1},{4,2},{5,3},{6,4},{7,5},{8,14},{9,15},{10,... | collective-permute-start | bytes 3145736 | tf_op jit(solution)/shard_map/ppermute | solution.py:135
  119.9 50.8 %collective-permute-start.2 = (f16[256,2048]{1,0:T(8,128)(2,1)S(1)}, f16[256,2048]{1,0:T(8,128)(2,1)S(1)}, u32[]{:S(2)}, u32[]{:S(2)}) collective-permute-start(f16[256,2048]{1,0:T(8,128)(2,1)S(1)} %fusion.80), channel_id=1, source_target_pairs={{0,1},{1,0},{2,3},{3,2},{4,5},{5,4},{6,7},{7,6},{8,9},{9,8},{10,11... | collective-permute-start | bytes 3145736 | tf_op jit(solution)/shard_map/ppermute | solution.py:120
  141.2 47.6 %collective-permute-start.7 = (f16[256,2048]{1,0:T(8,128)(2,1)S(1)}, f16[256,2048]{1,0:T(8,128)(2,1)S(1)}, u32[]{:S(2)}, u32[]{:S(2)}) collective-permute-start(f16[256,2048]{1,0:T(8,128)(2,1)S(1)} %fusion.168), channel_id=1, source_target_pairs={{0,2},{1,3},{2,4},{3,5},{4,6},{5,7},{6,0},{7,1},{8,10},{9,11},{10,... | collective-permute-start | bytes 3145736 | tf_op jit(solution)/shard_map/ppermute | solution.py:135
  162.7 46.9 %collective-permute-start.13 = (f16[256,2048]{1,0:T(8,128)(2,1)S(1)}, f16[256,2048]{1,0:T(8,128)(2,1)S(1)}, u32[]{:S(2)}, u32[]{:S(2)}) collective-permute-start(f16[256,2048]{1,0:T(8,128)(2,1)S(1)} %fusion.170), channel_id=1, source_target_pairs={{0,6},{1,7},{2,0},{3,1},{4,2},{5,3},{6,4},{7,5},{8,14},{9,15},{10,... | collective-permute-start | bytes 3145736 | tf_op jit(solution)/shard_map/ppermute | solution.py:135
  245.5 164.5 %all-gather.7.cloned.1.call-start = ((), (), s32[]{:S(2)}) async-start(), calls=%async_computation.1 | async-start | bytes 9437184 | tf_op jit(solution)/shard_map/all_gather | solution.py:165
  265.3 2.0 copy-start.1
Sparse Core Ops, SparseCore 0:
  245.6 82.1 all-gather.4
  329.4 80.5 all-gather.6
